TPU v7x, 32 devices: a whole 2x2x4 slice. The times are simulated.
32 devices in a mesh: wide: 16 (over z, x, core), narrow: 2 (over y).
Axes of the slice: x: 2, y: 2, z: 4, core: 2. Of those that a mesh axis runs over, the one named last changes fastest.
Arguments:
- vectors: float32 [1024, 16384], P('narrow', 'wide'), may hold values from -6 to 6
- weights: bfloat16 [5, 64, 256, 512], P(None, 'wide', 'narrow'), may hold values from -0.25 to 0.25
Outputs:
- transformed: float32 [1024, 16384], P('narrow', 'wide')
All inputs are finite; a program needn't handle non-finite values.
Results may differ from a plain program's by a relative error of at most 0.0003.
Values may be sent and summed in bfloat16 or wider, within the bound.
A program may use at most 64 MiB of HBM per device.

v0:
```python
import functools

import jax
import jax.numpy as jnp
from jax import lax
from jax.experimental import pallas as pl
from jax.experimental.pallas import tpu as pltpu
from jax.sharding import PartitionSpec as P

MESH = pl.DeviceIdType.MESH
POWER = 12
TOP = 2.0 ** (126 / POWER)
TINY = 1e-35
TILE = 256
WINDOW = 5
BF16 = jnp.bfloat16
F32 = jnp.float32

WEIGHT_ORDER = (
    (0, 0), (0, 2), (1, 0), (2, 0), (1, 2), (2, 2), (3, 0), (0, 1),
    (0, 3), (1, 1), (2, 1), (3, 2), (1, 3), (2, 3), (3, 1), (3, 3),
    (4, 0), (4, 2), (4, 1), (4, 3),
)
COMPUTE_ORDER = (
    (0, 0), (0, 2), (1, 0), (1, 2), (2, 0), (2, 2), (3, 0), (0, 1), (0, 3),
    (1, 1), (2, 1), (3, 2), (1, 3), (2, 3), (3, 1), (3, 3),
    (4, 0), (4, 2), (4, 1), (4, 3),
)


def split(value):
    high = value.astype(BF16)
    return high, (value - high.astype(F32)).astype(BF16)


def encode(value):
    scale = jnp.maximum(jnp.max(jnp.abs(value), axis=0, keepdims=True), TINY)
    t = value * (TOP / scale)
    t2 = t * t
    t4 = t2 * t2
    t12 = t4 * t4 * t4
    return jnp.where(t < 0, -t12, t12).astype(BF16), scale


def decode(code, scale):
    wide = code.astype(F32)
    size = jnp.exp(jnp.log(jnp.abs(wide)) * (1.0 / POWER)) * (scale * (1.0 / TOP))
    return jnp.where(wide == 0, 0.0, jnp.where(wide < 0, -size, size))


def kernel(
    peers, strides, x_hbm, w_hbm, out,
    x, w, l0, l1, l1_in, l2, z1_out, z1_in, s1_out, s1_in, l3, z2_out, z2_in, s2_out, s2_in,
    x_sem, own_sem, w_send, w_recv, core_send, core_recv, z_send, z_recv, s_send, s_recv,
):
    columns = x.shape[0]
    size = w.shape[3] // 2
    rows = w_hbm.shape[2]
    blocks = w.shape[1]
    tiles = columns // TILE
    me_n = lax.axis_index("narrow")
    me_w = lax.axis_index("wide")
    sides = [me_w // stride % 2 for stride in strides]
    partners = [me_w + (1 - 2 * side) * stride for side, stride in zip(sides, strides)]

    def x_copy(half):
        span = pl.ds(half * 2 * size, 2 * size)
        return pltpu.make_async_copy(x_hbm.at[:, span], x.at[:, span], x_sem.at[half])

    def own_copy(level, block):
        span = pl.ds(pl.multiple_of(me_n * rows, rows), rows)
        return pltpu.make_async_copy(
            w_hbm.at[level, block], w.at[level, block, span], own_sem.at[level, block]
        )

    def weight_copy(level, block, k, owner):
        span = pl.ds(pl.multiple_of(owner * rows, rows), rows)
        return pltpu.make_async_remote_copy(
            src_ref=w_hbm.at[level, block],
            dst_ref=w.at[level, block, span],
            send_sem=w_send.at[level, block, k - 1],
            recv_sem=w_recv.at[level, block, k - 1],
            device_id={"narrow": lax.rem(me_n + k, peers)},
            device_id_type=MESH,
        )

    def send_weight(position):
        if position < len(WEIGHT_ORDER):
            level, block = WEIGHT_ORDER[position]
            for k in range(1, peers):
                weight_copy(level, block, k, me_n).start()

    def core_copy(block):
        return pltpu.make_async_remote_copy(
            src_ref=l1.at[block], dst_ref=l1_in.at[block],
            send_sem=core_send.at[block], recv_sem=core_recv.at[block],
            device_id={"wide": partners[0]}, device_id_type=MESH,
        )

    def code_copies(level, block, tile):
        source, target = ((z1_out, z1_in), (z2_out, z2_in))[level]
        s_source, s_target = ((s1_out, s1_in), (s2_out, s2_in))[level]
        partner = partners[level + 1]
        return (
            pltpu.make_async_remote_copy(
                src_ref=s_source.at[block, tile], dst_ref=s_target.at[block, tile],
                send_sem=s_send.at[level, block, tile], recv_sem=s_recv.at[level, block, tile],
                device_id={"wide": partner}, device_id_type=MESH,
            ),
            pltpu.make_async_remote_copy(
                src_ref=source.at[block, at_tile(tile)], dst_ref=target.at[block, at_tile(tile)],
                send_sem=z_send.at[level, block, tile], recv_sem=z_recv.at[level, block, tile],
                device_id={"wide": partner}, device_id_type=MESH,
            ),
        )

    def product(level, block, first, second, side, finish):
        def step(tile, carry):
            total = None
            for part, half in ((first, side), (second, 1 - side)):
                start = half * size
                if not isinstance(half, int):
                    start = pl.multiple_of(start, size)
                matrix = w[level, block, :, pl.ds(start, size)]
                lhs = jnp.concatenate(part(tile), axis=0)
                term = lax.dot_general(
                    lhs, matrix, (((1,), (1,)), ((), ())), preferred_element_type=F32
                )
                total = term if total is None else total + term
            finish(tile, total[:TILE] + total[TILE:])
            return carry

        lax.fori_loop(0, tiles, step, 0)

    def at_tile(tile):
        return pl.ds(pl.multiple_of(tile * TILE, TILE), TILE)

    def from_x(block):
        return lambda tile: split(x[at_tile(tile), pl.ds(block * size, size)])

    def from_pair(ref, block):
        return lambda tile: (ref[block, 0, at_tile(tile)], ref[block, 1, at_tile(tile)])

    def from_code(level, block):
        ref, scales = ((z1_in, s1_in), (z2_in, s2_in))[level]

        def load(tile):
            for copy in code_copies(level, block, tile):
                copy.wait_recv()
            return split(decode(ref[block, at_tile(tile)], scales[block, tile]))

        return load

    def to_pair(ref, block):
        def finish(tile, value):
            high, low = split(value)
            ref[block, 0, at_tile(tile)] = high
            ref[block, 1, at_tile(tile)] = low

        return finish

    def to_code(level, block):
        keep = to_pair((l2, l3)[level], block)
        code_ref, scale_ref = ((z1_out, s1_out), (z2_out, s2_out))[level]

        def finish(tile, value):
            keep(tile, value)
            code, scale = encode(value)
            code_ref[block, at_tile(tile)] = code
            scale_ref[block, tile] = scale
            for copy in code_copies(level, block, tile):
                copy.start()

        return finish

    def to_out(block):
        def finish(tile, value):
            out[at_tile(tile), pl.ds(block * size, size)] = value

        return finish

    for half in range(blocks // 2):
        x_copy(half).start()
    for level, block in WEIGHT_ORDER:
        own_copy(level, block).start()

    barrier = pltpu.get_barrier_semaphore()
    for k in range(1, peers):
        pl.semaphore_signal(
            barrier, inc=1, device_id={"narrow": lax.rem(me_n + k, peers)}, device_id_type=MESH
        )
    for partner in partners:
        pl.semaphore_signal(barrier, inc=1, device_id={"wide": partner}, device_id_type=MESH)
    pl.semaphore_wait(barrier, peers - 1 + len(partners))

    for position in range(WINDOW):
        send_weight(position)

    arrived = [0]

    def need_weight(level, block):
        while (level, block) in WEIGHT_ORDER[arrived[0]:]:
            next_level, next_block = WEIGHT_ORDER[arrived[0]]
            own_copy(next_level, next_block).wait()
            for k in range(1, peers):
                weight_copy(
                    next_level, next_block, k, lax.rem(me_n + peers - k, peers)
                ).wait_recv()
            send_weight(arrived[0] + WINDOW)
            arrived[0] += 1

    x_ready = set()
    for level, block in COMPUTE_ORDER:
        if level == 0 and block // 2 not in x_ready:
            x_copy(block // 2).wait()
            x_ready.add(block // 2)
        need_weight(level, block)
        if level < 2:
            stride = 1 << level
            low = block - block // stride % 2 * stride
            high = low + stride
        if level == 0:
            product(level, block, from_x(low), from_x(high), 0, to_pair(l0, block))
        elif level == 1:
            product(level, block, from_pair(l0, low), from_pair(l0, high), 0, to_pair(l1, block))
            core_copy(block).start()
        elif level == 2:
            core_copy(block).wait_recv()
            product(
                level, block, from_pair(l1, block), from_pair(l1_in, block), sides[0],
                to_code(0, block),
            )
        elif level == 3:
            product(
                level, block, from_pair(l2, block), from_code(0, block), sides[1],
                to_code(1, block),
            )
        else:
            product(
                level, block, from_pair(l3, block), from_code(1, block), sides[2], to_out(block)
            )

    for level, block in WEIGHT_ORDER:
        for k in range(1, peers):
            weight_copy(level, block, k, me_n).wait_send()
    for block in range(blocks):
        core_copy(block).wait_send()
        for level in range(2):
            for tile in range(tiles):
                for copy in code_copies(level, block, tile):
                    copy.wait_send()


def on_device(vectors, weights):
    columns, coeffs = vectors.shape
    levels, blocks, rows, depth = weights.shape
    size = depth // 2
    peers = lax.axis_size("narrow")
    wide_top = lax.axis_size("wide").bit_length() - 1
    strides = [1 << bit for bit in (0, wide_top // 2, wide_top - 1)]
    tiles = columns // TILE
    pair = pltpu.VMEM((blocks, 2, columns, size), BF16)
    code = pltpu.VMEM((blocks, columns, size), BF16)
    scale = pltpu.VMEM((blocks, tiles, 1, size), F32)
    dma = pltpu.SemaphoreType.DMA
    return pl.pallas_call(
        functools.partial(kernel, peers, strides),
        out_shape=pltpu.VMEM((columns, coeffs), F32),
        in_specs=[pl.BlockSpec(memory_space=pltpu.HBM)] * 2,
        out_specs=pl.BlockSpec(memory_space=pltpu.VMEM),
        scratch_shapes=[
            pltpu.VMEM((columns, coeffs), F32),
            pltpu.VMEM((levels, blocks, size, depth), BF16),
            pair, pair, pair, pair,
            code, code, scale, scale,
            pair,
            code, code, scale, scale,
            dma((blocks // 2,)),
            dma((levels, blocks)),
            dma((levels, blocks, max(peers - 1, 1))),
            dma((levels, blocks, max(peers - 1, 1))),
            dma((blocks,)),
            dma((blocks,)),
            dma((2, blocks, tiles)),
            dma((2, blocks, tiles)),
            dma((2, blocks, tiles)),
            dma((2, blocks, tiles)),
        ],
        compiler_params=pltpu.CompilerParams(
            collective_id=0, has_side_effects=True, vmem_limit_bytes=40 * 1024 * 1024
        ),
    )(vectors, weights)


def solution(mesh):
    placed = (P("narrow", "wide"), P(None, "wide", "narrow", None))
    return jax.shard_map(
        on_device, mesh=mesh, in_specs=placed, out_specs=P("narrow", "wide"), check_vma=False
    )
```

profile of v0, /device:TPU:0, one launch (start us, length us, event | category | flops | bytes accessed | tf_op | source)
XLA Modules:
  0.0 85.9 jit_solution(13520266980982360820)
XLA Ops:
  0.0 0.0 copy-start
  0.0 1.7 %copy-done = bf16[5,4,128,512]{3,2,1,0:T(8,128)(2,1)S(1)} copy-done((bf16[5,4,128,512]{3,2,1,0:T(8,128)(2,1)S(1)}, bf16[5,4,128,512]{3,2,1,0:T(8,128)(2,1)}, u32[]{:S(2)}) %copy-start) | copy-done | bytes 2621464
  1.7 0.0 copy-start.1
  1.7 1.6 %copy-done.1 = f32[512,1024]{1,0:T(8,128)S(1)} copy-done((f32[512,1024]{1,0:T(8,128)S(1)}, f32[512,1024]{1,0:T(8,128)}, u32[]{:S(2)}) %copy-start.1) | copy-done | bytes 2097176
  3.3 81.2 %shard_map.28 = f32[512,1024]{1,0:T(8,128)S(1)} custom-call(f32[512,1024]{1,0:T(8,128)S(1)} %copy-done.1, bf16[5,4,128,512]{3,2,1,0:T(8,128)(2,1)S(1)} %copy-done), custom_call_target="tpu_custom_call" | custom-call | tf_op jit(solution)/shard_map/pallas_call | solution.py:266
  84.6 1.3 %copy.4 = f32[512,1024]{1,0:T(8,128)} copy(f32[512,1024]{1,0:T(8,128)S(1)} %shard_map.28) | data formatting | bytes 4194304
Async XLA Ops:
  0.0 1.7 %copy-start = (bf16[5,4,128,512]{3,2,1,0:T(8,128)(2,1)S(1)}, bf16[5,4,128,512]{3,2,1,0:T(8,128)(2,1)}, u32[]{:S(2)}) copy-start(bf16[5,4,128,512]{3,2,1,0:T(8,128)(2,1)} %w_hbm.1) | copy-start | bytes 7864324
  1.7 1.6 %copy-start.1 = (f32[512,1024]{1,0:T(8,128)S(1)}, f32[512,1024]{1,0:T(8,128)}, u32[]{:S(2)}) copy-start(f32[512,1024]{1,0:T(8,128)} %x_hbm.1) | copy-start | bytes 6291460
where the time goes:
time: 86.1 us; the launch traced here: 85.9 us
  Pallas kernels  81.2 us (94%)
  local copies, waits for them, and re-layouts  4.65 us (5%)
    pallas_call x1, Pallas kernels, on_device(): pl.pallas_call(functools.partial(kernel, peers, strides), out_shape=pltpu...  81.2 us
    unnamed x5, local copies, waits for them, and re-layouts  4.65 us

commit v1 on v0

--- a/solution.py
+++ b/solution.py
@@ -11,20 +11,24 @@
 POWER = 12
 TOP = 2.0 ** (126 / POWER)
 TINY = 1e-35
-TILE = 256
-WINDOW = 5
+TILE = 128
+LOCAL_TILE = 256
+WINDOW = 8
 BF16 = jnp.bfloat16
 F32 = jnp.float32
 
 WEIGHT_ORDER = (
-    (0, 0), (0, 2), (1, 0), (2, 0), (1, 2), (2, 2), (3, 0), (0, 1),
-    (0, 3), (1, 1), (2, 1), (3, 2), (1, 3), (2, 3), (3, 1), (3, 3),
-    (4, 0), (4, 2), (4, 1), (4, 3),
+    (0, 0), (0, 2), (1, 0), (2, 0), (3, 0), (1, 2), (2, 2), (0, 1), (3, 2), (0, 3),
+    (1, 1), (2, 1), (3, 1), (1, 3), (2, 3), (3, 3), (4, 0), (4, 2), (4, 1), (4, 3),
 )
-COMPUTE_ORDER = (
-    (0, 0), (0, 2), (1, 0), (1, 2), (2, 0), (2, 2), (3, 0), (0, 1), (0, 3),
-    (1, 1), (2, 1), (3, 2), (1, 3), (2, 3), (3, 1), (3, 3),
-    (4, 0), (4, 2), (4, 1), (4, 3),
+STEPS = (
+    ("run", 0, 0, 0, 4), ("run", 0, 2, 0, 4), ("run", 1, 0, 0, 4), ("run", 2, 0, 0, 4),
+    ("run", 3, 0, 0, 2), ("run", 1, 2, 0, 4), ("hold", 3, 0, 2, 4), ("run", 2, 2, 0, 4),
+    ("send", 3, 0, 2, 4), ("run", 0, 1, 0, 4), ("run", 3, 2, 0, 2), ("run", 0, 3, 0, 4),
+    ("hold", 3, 2, 2, 4), ("run", 1, 1, 0, 4), ("run", 2, 1, 0, 4), ("send", 3, 2, 2, 4),
+    ("run", 3, 1, 0, 2), ("run", 1, 3, 0, 4), ("hold", 3, 1, 2, 4), ("run", 2, 3, 0, 4),
+    ("send", 3, 1, 2, 4), ("run", 3, 3, 0, 4), ("run", 4, 0, 0, 4), ("run", 4, 2, 0, 4),
+    ("run", 4, 1, 0, 4), ("run", 4, 3, 0, 4),
 )
 
 
@@ -61,23 +65,25 @@
     me_n = lax.axis_index("narrow")
     me_w = lax.axis_index("wide")
     sides = [me_w // stride % 2 for stride in strides]
+    same_way = sides[1] == sides[2]
     partners = [me_w + (1 - 2 * side) * stride for side, stride in zip(sides, strides)]
 
     def x_copy(half):
         span = pl.ds(half * 2 * size, 2 * size)
         return pltpu.make_async_copy(x_hbm.at[:, span], x.at[:, span], x_sem.at[half])
 
+    def rows_of(owner):
+        return pl.ds(pl.multiple_of(owner * rows, rows), rows)
+
     def own_copy(level, block):
-        span = pl.ds(pl.multiple_of(me_n * rows, rows), rows)
         return pltpu.make_async_copy(
-            w_hbm.at[level, block], w.at[level, block, span], own_sem.at[level, block]
+            w_hbm.at[level, block], w.at[level, block, rows_of(me_n)], own_sem.at[level, block]
         )
 
     def weight_copy(level, block, k, owner):
-        span = pl.ds(pl.multiple_of(owner * rows, rows), rows)
         return pltpu.make_async_remote_copy(
-            src_ref=w_hbm.at[level, block],
-            dst_ref=w.at[level, block, span],
+            src_ref=w.at[level, block, rows_of(owner)],
+            dst_ref=w.at[level, block, rows_of(owner)],
             send_sem=w_send.at[level, block, k - 1],
             recv_sem=w_recv.at[level, block, k - 1],
             device_id={"narrow": lax.rem(me_n + k, peers)},
@@ -87,13 +93,14 @@
     def send_weight(position):
         if position < len(WEIGHT_ORDER):
             level, block = WEIGHT_ORDER[position]
+            own_copy(level, block).wait()
             for k in range(1, peers):
                 weight_copy(level, block, k, me_n).start()
 
-    def core_copy(block):
+    def core_copy(block, tile):
         return pltpu.make_async_remote_copy(
-            src_ref=l1.at[block], dst_ref=l1_in.at[block],
-            send_sem=core_send.at[block], recv_sem=core_recv.at[block],
+            src_ref=l1.at[block, :, at_tile(tile)], dst_ref=l1_in.at[block, :, at_tile(tile)],
+            send_sem=core_send.at[block, tile], recv_sem=core_recv.at[block, tile],
             device_id={"wide": partners[0]}, device_id_type=MESH,
         )
 
@@ -114,7 +121,11 @@
             ),
         )
 
-    def product(level, block, first, second, side, finish):
+    def send_codes(level, block, tile):
+        for copy in code_copies(level, block, tile):
+            copy.start()
+
+    def product(level, block, first, second, side, finish, span, height=TILE):
         def step(tile, carry):
             total = None
             for part, half in ((first, side), (second, 1 - side)):
@@ -127,19 +138,30 @@
                     lhs, matrix, (((1,), (1,)), ((), ())), preferred_element_type=F32
                 )
                 total = term if total is None else total + term
-            finish(tile, total[:TILE] + total[TILE:])
+            finish(tile, total[:height] + total[height:])
             return carry
 
-        lax.fori_loop(0, tiles, step, 0)
-
-    def at_tile(tile):
-        return pl.ds(pl.multiple_of(tile * TILE, TILE), TILE)
+        lax.fori_loop(*span, step, 0)
+
+    def at_tile(tile, height=TILE):
+        return pl.ds(pl.multiple_of(tile * height, height), height)
 
     def from_x(block):
-        return lambda tile: split(x[at_tile(tile), pl.ds(block * size, size)])
-
-    def from_pair(ref, block):
-        return lambda tile: (ref[block, 0, at_tile(tile)], ref[block, 1, at_tile(tile)])
+        return lambda tile: split(x[at_tile(tile, LOCAL_TILE), pl.ds(block * size, size)])
+
+    def from_pair(ref, block, height=TILE):
+        return lambda tile: (
+            ref[block, 0, at_tile(tile, height)], ref[block, 1, at_tile(tile, height)]
+        )
+
+    def from_core(block):
+        load = from_pair(l1_in, block)
+
+        def wait_and_load(tile):
+            core_copy(block, tile).wait_recv()
+            return load(tile)
+
+        return wait_and_load
 
     def from_code(level, block):
         ref, scales = ((z1_in, s1_in), (z2_in, s2_in))[level]
@@ -151,25 +173,38 @@
 
         return load
 
-    def to_pair(ref, block):
+    def to_pair(ref, block, height=TILE):
         def finish(tile, value):
             high, low = split(value)
-            ref[block, 0, at_tile(tile)] = high
-            ref[block, 1, at_tile(tile)] = low
+            ref[block, 0, at_tile(tile, height)] = high
+            ref[block, 1, at_tile(tile, height)] = low
 
         return finish
 
-    def to_code(level, block):
+    def to_core(block):
+        keep = to_pair(l1, block, LOCAL_TILE)
+        pieces = LOCAL_TILE // TILE
+
+        def finish(tile, value):
+            keep(tile, value)
+            for piece in range(pieces):
+                core_copy(block, tile * pieces + piece).start()
+
+        return finish
+
+    def to_code(level, block, held):
         keep = to_pair((l2, l3)[level], block)
         code_ref, scale_ref = ((z1_out, s1_out), (z2_out, s2_out))[level]
 
         def finish(tile, value):
-            keep(tile, value)
             code, scale = encode(value)
             code_ref[block, at_tile(tile)] = code
             scale_ref[block, tile] = scale
-            for copy in code_copies(level, block, tile):
-                copy.start()
+            if held:
+                pl.when(jnp.logical_not(same_way))(lambda: send_codes(level, block, tile))
+            else:
+                send_codes(level, block, tile)
+            keep(tile, value)
 
         return finish
 
@@ -179,9 +214,12 @@
 
         return finish
 
-    for half in range(blocks // 2):
+    x_copy(0).start()
+    for level, block in WEIGHT_ORDER[:WINDOW]:
+        own_copy(level, block).start()
+    for half in range(1, blocks // 2):
         x_copy(half).start()
-    for level, block in WEIGHT_ORDER:
+    for level, block in WEIGHT_ORDER[WINDOW:]:
         own_copy(level, block).start()
 
     barrier = pltpu.get_barrier_semaphore()
@@ -201,7 +239,6 @@
     def need_weight(level, block):
         while (level, block) in WEIGHT_ORDER[arrived[0]:]:
             next_level, next_block = WEIGHT_ORDER[arrived[0]]
-            own_copy(next_level, next_block).wait()
             for k in range(1, peers):
                 weight_copy(
                     next_level, next_block, k, lax.rem(me_n + peers - k, peers)
@@ -210,7 +247,20 @@
             arrived[0] += 1
 
     x_ready = set()
-    for level, block in COMPUTE_ORDER:
+    local = (0, columns // LOCAL_TILE)
+    share = tiles // 4
+    for kind, level, block, start, stop in STEPS:
+        span = (start * share, stop * share)
+        if kind == "send":
+            @pl.when(same_way)
+            def _():
+                def send(tile, carry):
+                    send_codes(level - 2, block, tile)
+                    return carry
+
+                lax.fori_loop(*span, send, 0)
+
+            continue
         if level == 0 and block // 2 not in x_ready:
             x_copy(block // 2).wait()
             x_ready.add(block // 2)
@@ -220,33 +270,38 @@
             low = block - block // stride % 2 * stride
             high = low + stride
         if level == 0:
-            product(level, block, from_x(low), from_x(high), 0, to_pair(l0, block))
+            product(
+                level, block, from_x(low), from_x(high), 0, to_pair(l0, block, LOCAL_TILE),
+                local, LOCAL_TILE,
+            )
         elif level == 1:
-            product(level, block, from_pair(l0, low), from_pair(l0, high), 0, to_pair(l1, block))
-            core_copy(block).start()
+            product(
+                level, block, from_pair(l0, low, LOCAL_TILE), from_pair(l0, high, LOCAL_TILE), 0,
+                to_core(block), local, LOCAL_TILE,
+            )
         elif level == 2:
-            core_copy(block).wait_recv()
-            product(
-                level, block, from_pair(l1, block), from_pair(l1_in, block), sides[0],
-                to_code(0, block),
+            product(
+                level, block, from_pair(l1, block), from_core(block), sides[0],
+                to_code(0, block, kind == "hold"), span,
             )
         elif level == 3:
             product(
                 level, block, from_pair(l2, block), from_code(0, block), sides[1],
-                to_code(1, block),
+                to_code(1, block, kind == "hold"), span,
             )
         else:
             product(
-                level, block, from_pair(l3, block), from_code(1, block), sides[2], to_out(block)
+                level, block, from_pair(l3, block), from_code(1, block), sides[2],
+                to_out(block), span,
             )
 
     for level, block in WEIGHT_ORDER:
         for k in range(1, peers):
             weight_copy(level, block, k, me_n).wait_send()
     for block in range(blocks):
-        core_copy(block).wait_send()
-        for level in range(2):
-            for tile in range(tiles):
+        for tile in range(tiles):
+            core_copy(block, tile).wait_send()
+            for level in range(2):
                 for copy in code_copies(level, block, tile):
                     copy.wait_send()
 
@@ -279,15 +334,15 @@
             dma((levels, blocks)),
             dma((levels, blocks, max(peers - 1, 1))),
             dma((levels, blocks, max(peers - 1, 1))),
-            dma((blocks,)),
-            dma((blocks,)),
+            dma((blocks, tiles)),
+            dma((blocks, tiles)),
             dma((2, blocks, tiles)),
             dma((2, blocks, tiles)),
             dma((2, blocks, tiles)),
             dma((2, blocks, tiles)),
         ],
         compiler_params=pltpu.CompilerParams(
-            collective_id=0, has_side_effects=True, vmem_limit_bytes=40 * 1024 * 1024
+            collective_id=0, has_side_effects=True, vmem_limit_bytes=61 * 1024 * 1024
         ),
     )(vectors, weights)
 

time: 86.1 us -> 77.4 us (0.90)
  Pallas kernels: 81.2 us -> 75.9 us
  local copies, waits for them, and re-layouts: 4.65 us -> 1.32 us
    pallas_call x1, Pallas kernels: 81.2 us -> 75.9 us  [on_device(): pl.pallas_call(functools.partial(kernel, peers, strides), out_shape=pltpu...]
    unnamed x5 -> x1, local copies, waits for them, and re-layouts: 4.65 us -> 1.32 us
where the time goes in v1:
time: 77.4 us; the launch traced here: 77.2 us
  Pallas kernels  75.9 us (98%)
  local copies, waits for them, and re-layouts  1.32 us (2%)
    pallas_call x1, Pallas kernels, on_device(): pl.pallas_call(functools.partial(kernel, peers, strides), out_shape=pltpu...  75.9 us

profile of v1, /device:TPU:0, one launch (start us, length us, event | category | flops | bytes accessed | tf_op | source)
XLA Modules:
  0.0 77.2 jit_solution(7403527519428294807)
XLA Ops:
  0.0 75.9 %shard_map.28 = f32[512,1024]{1,0:T(8,128)S(1)} custom-call(f32[512,1024]{1,0:T(8,128)} %x_hbm.1, bf16[5,4,128,512]{3,2,1,0:T(8,128)(2,1)} %w_hbm.1), custom_call_target="tpu_custom_call" | custom-call | tf_op jit(solution)/shard_map/pallas_call | solution.py:321
  75.9 1.3 %copy.4 = f32[512,1024]{1,0:T(8,128)} copy(f32[512,1024]{1,0:T(8,128)S(1)} %shard_map.28) | data formatting | bytes 4194304

commit v2 on v1

--- a/solution.py
+++ b/solution.py
@@ -19,15 +19,15 @@
 
 WEIGHT_ORDER = (
     (0, 0), (0, 2), (1, 0), (2, 0), (3, 0), (1, 2), (2, 2), (0, 1), (3, 2), (0, 3),
-    (1, 1), (2, 1), (3, 1), (1, 3), (2, 3), (3, 3), (4, 0), (4, 2), (4, 1), (4, 3),
+    (1, 1), (2, 1), (3, 1), (1, 3), (2, 3), (4, 0), (3, 3), (4, 2), (4, 1), (4, 3),
 )
 STEPS = (
     ("run", 0, 0, 0, 4), ("run", 0, 2, 0, 4), ("run", 1, 0, 0, 4), ("run", 2, 0, 0, 4),
     ("run", 3, 0, 0, 2), ("run", 1, 2, 0, 4), ("hold", 3, 0, 2, 4), ("run", 2, 2, 0, 4),
     ("send", 3, 0, 2, 4), ("run", 0, 1, 0, 4), ("run", 3, 2, 0, 2), ("run", 0, 3, 0, 4),
-    ("hold", 3, 2, 2, 4), ("run", 1, 1, 0, 4), ("run", 2, 1, 0, 4), ("send", 3, 2, 2, 4),
-    ("run", 3, 1, 0, 2), ("run", 1, 3, 0, 4), ("hold", 3, 1, 2, 4), ("run", 2, 3, 0, 4),
-    ("send", 3, 1, 2, 4), ("run", 3, 3, 0, 4), ("run", 4, 0, 0, 4), ("run", 4, 2, 0, 4),
+    ("run", 1, 1, 0, 4), ("run", 3, 2, 2, 4), ("run", 2, 1, 0, 4), ("run", 1, 3, 0, 4),
+    ("run", 3, 1, 0, 2), ("run", 2, 3, 0, 4), ("run", 3, 1, 2, 4), ("run", 3, 3, 0, 2),
+    ("run", 4, 0, 0, 4), ("run", 4, 2, 0, 4), ("run", 3, 3, 2, 4), ("drain", 0, 0, 0, 4),
     ("run", 4, 1, 0, 4), ("run", 4, 3, 0, 4),
 )
 
@@ -192,7 +192,7 @@
 
         return finish
 
-    def to_code(level, block, held):
+    def to_code(level, block, kind):
         keep = to_pair((l2, l3)[level], block)
         code_ref, scale_ref = ((z1_out, s1_out), (z2_out, s2_out))[level]
 
@@ -200,9 +200,11 @@
             code, scale = encode(value)
             code_ref[block, at_tile(tile)] = code
             scale_ref[block, tile] = scale
-            if held:
+            if kind == "hold":
                 pl.when(jnp.logical_not(same_way))(lambda: send_codes(level, block, tile))
-            else:
+            elif kind == "holdi":
+                pl.when(same_way)(lambda: send_codes(level, block, tile))
+            elif kind == "run":
                 send_codes(level, block, tile)
             keep(tile, value)
 
@@ -214,13 +216,11 @@
 
         return finish
 
-    x_copy(0).start()
-    for level, block in WEIGHT_ORDER[:WINDOW]:
+    for position, (level, block) in enumerate(WEIGHT_ORDER):
         own_copy(level, block).start()
-    for half in range(1, blocks // 2):
-        x_copy(half).start()
-    for level, block in WEIGHT_ORDER[WINDOW:]:
-        own_copy(level, block).start()
+        if position in (0, 4):
+            for half in range(position // 4, blocks // 2 if position else 1):
+                x_copy(half).start()
 
     barrier = pltpu.get_barrier_semaphore()
     for k in range(1, peers):
@@ -251,8 +251,18 @@
     share = tiles // 4
     for kind, level, block, start, stop in STEPS:
         span = (start * share, stop * share)
-        if kind == "send":
-            @pl.when(same_way)
+        if kind == "drain":
+            for level, block in WEIGHT_ORDER:
+                for k in range(1, peers):
+                    weight_copy(level, block, k, me_n).wait_send()
+            for block in range(blocks):
+                for tile in range(tiles):
+                    core_copy(block, tile).wait_send()
+                    for copy in code_copies(0, block, tile):
+                        copy.wait_send()
+            continue
+        if kind.startswith("send"):
+            @pl.when({"send": same_way, "sendi": jnp.logical_not(same_way), "senda": True}[kind])
             def _():
                 def send(tile, carry):
                     send_codes(level - 2, block, tile)
@@ -282,12 +292,12 @@
         elif level == 2:
             product(
                 level, block, from_pair(l1, block), from_core(block), sides[0],
-                to_code(0, block, kind == "hold"), span,
+                to_code(0, block, kind), span,
             )
         elif level == 3:
             product(
                 level, block, from_pair(l2, block), from_code(0, block), sides[1],
-                to_code(1, block, kind == "hold"), span,
+                to_code(1, block, kind), span,
             )
         else:
             product(
@@ -295,15 +305,10 @@
                 to_out(block), span,
             )
 
-    for level, block in WEIGHT_ORDER:
-        for k in range(1, peers):
-            weight_copy(level, block, k, me_n).wait_send()
     for block in range(blocks):
         for tile in range(tiles):
-            core_copy(block, tile).wait_send()
-            for level in range(2):
-                for copy in code_copies(level, block, tile):
-                    copy.wait_send()
+            for copy in code_copies(1, block, tile):
+                copy.wait_send()
 
 
 def on_device(vectors, weights):

time: 77.4 us -> 73.7 us (0.952)
  Pallas kernels: 75.9 us -> 72.2 us
    pallas_call x1, Pallas kernels: 75.9 us -> 72.2 us  [on_device(): pl.pallas_call(functools.partial(kernel, peers, strides), out_shape=pltpu...]
where the time goes in v2:
time: 73.7 us; the launch traced here: 73.5 us
  Pallas kernels  72.2 us (98%)
  local copies, waits for them, and re-layouts  1.32 us (2%)
    pallas_call x1, Pallas kernels, on_device(): pl.pallas_call(functools.partial(kernel, peers, strides), out_shape=pltpu...  72.2 us

profile of v2, /device:TPU:0, one launch (start us, length us, event | category | flops | bytes accessed | tf_op | source)
XLA Modules:
  0.0 73.5 jit_solution(6447814577182353311)
XLA Ops:
  0.0 72.2 %shard_map.28 = f32[512,1024]{1,0:T(8,128)S(1)} custom-call(f32[512,1024]{1,0:T(8,128)} %x_hbm.1, bf16[5,4,128,512]{3,2,1,0:T(8,128)(2,1)} %w_hbm.1), custom_call_target="tpu_custom_call" | custom-call | tf_op jit(solution)/shard_map/pallas_call | solution.py:326
  72.2 1.3 %copy.4 = f32[512,1024]{1,0:T(8,128)} copy(f32[512,1024]{1,0:T(8,128)S(1)} %shard_map.28) | data formatting | bytes 4194304

commit v3 on v2

--- a/solution.py
+++ b/solution.py
@@ -25,10 +25,11 @@
     ("run", 0, 0, 0, 4), ("run", 0, 2, 0, 4), ("run", 1, 0, 0, 4), ("run", 2, 0, 0, 4),
     ("run", 3, 0, 0, 2), ("run", 1, 2, 0, 4), ("hold", 3, 0, 2, 4), ("run", 2, 2, 0, 4),
     ("send", 3, 0, 2, 4), ("run", 0, 1, 0, 4), ("run", 3, 2, 0, 2), ("run", 0, 3, 0, 4),
-    ("run", 1, 1, 0, 4), ("run", 3, 2, 2, 4), ("run", 2, 1, 0, 4), ("run", 1, 3, 0, 4),
+    ("run", 1, 1, 0, 4), ("holdi", 3, 2, 2, 3), ("holdi", 3, 2, 3, 4), ("run", 2, 1, 0, 2),
+    ("sendi", 3, 2, 2, 3), ("run", 2, 1, 2, 4), ("sendi", 3, 2, 3, 4), ("run", 1, 3, 0, 4),
     ("run", 3, 1, 0, 2), ("run", 2, 3, 0, 4), ("run", 3, 1, 2, 4), ("run", 3, 3, 0, 2),
     ("run", 4, 0, 0, 4), ("run", 4, 2, 0, 4), ("run", 3, 3, 2, 4), ("drain", 0, 0, 0, 4),
-    ("run", 4, 1, 0, 4), ("run", 4, 3, 0, 4),
+    ("tall", 4, 1, 0, 4), ("run", 4, 3, 0, 4),
 )
 
 
@@ -173,6 +174,16 @@
 
         return load
 
+    def from_codes(level, block):
+        load = from_code(level, block)
+        pieces = LOCAL_TILE // TILE
+
+        def load_tall(tile):
+            parts = [load(tile * pieces + piece) for piece in range(pieces)]
+            return [jnp.concatenate(part, axis=0) for part in zip(*parts)]
+
+        return load_tall
+
     def to_pair(ref, block, height=TILE):
         def finish(tile, value):
             high, low = split(value)
@@ -210,9 +221,9 @@
 
         return finish
 
-    def to_out(block):
+    def to_out(block, height=TILE):
         def finish(tile, value):
-            out[at_tile(tile), pl.ds(block * size, size)] = value
+            out[at_tile(tile, height), pl.ds(block * size, size)] = value
 
         return finish
 
@@ -298,6 +309,11 @@
             product(
                 level, block, from_pair(l2, block), from_code(0, block), sides[1],
                 to_code(1, block, kind), span,
+            )
+        elif kind == "tall":
+            product(
+                level, block, from_pair(l3, block, LOCAL_TILE), from_codes(1, block), sides[2],
+                to_out(block, LOCAL_TILE), local, LOCAL_TILE,
             )
         else:
             product(

time: 73.7 us -> 73.5 us (level)
  no operation moved by 1% of the time
where the time goes in v3:
time: 73.5 us; the launch traced here: 73.3 us
  Pallas kernels  72 us (98%)
  local copies, waits for them, and re-layouts  1.32 us (2%)
    pallas_call x1, Pallas kernels, on_device(): pl.pallas_call(functools.partial(kernel, peers, strides), out_shape=pltpu...  72 us

profile of v3, /device:TPU:0, one launch (start us, length us, event | category | flops | bytes accessed | tf_op | source)
XLA Modules:
  0.0 73.3 jit_solution(10772960735303966695)
XLA Ops:
  0.0 72.0 %shard_map.28 = f32[512,1024]{1,0:T(8,128)S(1)} custom-call(f32[512,1024]{1,0:T(8,128)} %x_hbm.1, bf16[5,4,128,512]{3,2,1,0:T(8,128)(2,1)} %w_hbm.1), custom_call_target="tpu_custom_call" | custom-call | tf_op jit(solution)/shard_map/pallas_call | solution.py:342
  72.0 1.3 %copy.4 = f32[512,1024]{1,0:T(8,128)} copy(f32[512,1024]{1,0:T(8,128)S(1)} %shard_map.28) | data formatting | bytes 4194304
